TPU v7x, 32 devices: a whole 2x2x4 slice. The times are simulated.
32 devices in a mesh: tau: 4 (over x, core), tile: 8 (over z, y).
Axes of the slice: x: 2, y: 2, z: 4, core: 2. Of those that a mesh axis runs over, the one named last changes fastest.
Arguments:
- occupied: bfloat16 [4, 1024, 128, 128], P('tau', 'tile'), may hold values from -6 to 6
- virtual: bfloat16 [4, 1024, 128, 128], P('tau', 'tile'), may hold values from -0.125 to 0.125
- cos_weights: float32 [4, 4], replicated, may hold values from -1 to 1
- pair_occ: int32 [1536, 16], P('tile'), may hold values from 0 to 127
- pair_virt: int32 [1536, 16], P('tile'), may hold values from 0 to 127
- partial_target_tile: int32 [1536], P('tile'), may hold values from 0 to 255, as said below
Outputs:
- spectrum: float32 [4, 256, 128, 128], P(None, 'tile', 'tau')
Inputs may be any that keep to these rules, and one draw needn't show every extreme that they name: `partial_target_tile`: within each aligned block of 192 entries, no owner (values d * 32 to (d + 1) * 32 - 1 for owner d) is named more than 48 times; one owner is named exactly 48 times in every block.
All inputs are finite; a program needn't handle non-finite values.
Results may differ from a plain program's by a relative error of at most 0.0003.
Values sent between devices are 32-bit elements; how exact they have to be, the bound alone decides.
A program may use at most 192 MiB of HBM per device.

v0:
```python
import math

import jax
import jax.numpy as jnp
from jax import lax
from jax.sharding import PartitionSpec as P

CHI_DEV = 32


def block_products(occupied, virtual, occ_index, virt_index, groups):
    tau_count = occupied.shape[0]
    tile_size = occupied.shape[2]
    rows = tile_size // groups
    part_count = occ_index.shape[0]
    terms = occ_index.shape[1]
    group = math.gcd(part_count, 8)
    count = part_count // group
    empty = jnp.zeros((groups, part_count, tau_count, rows, tile_size), jnp.float32)

    def one_block(block, result):
        first = block * group
        occ_rows = lax.dynamic_slice_in_dim(occ_index, first, group, 0)
        virt_rows = lax.dynamic_slice_in_dim(virt_index, first, group, 0)
        left = jnp.take(occupied[0], occ_rows, axis=0)
        right = jnp.take(virtual[0], virt_rows, axis=0)
        left = left.reshape(group, terms, groups, rows, tile_size)
        pieces = [jnp.einsum("bjgrk,bjkc->gbrc", left, right, preferred_element_type=jnp.float32)]
        stacked = jnp.stack(pieces, axis=2)
        return lax.dynamic_update_slice_in_dim(result, stacked, first, 1)

    return lax.fori_loop(0, count, one_block, empty)


def slot_layout(partial_target_tile, chi_dev, owners, capacity):
    owner = partial_target_tile // chi_dev
    member = (owner[:, None] == jnp.arange(owners, dtype=jnp.int32)[None, :]).astype(jnp.int32)
    before = jnp.cumsum(member, axis=0) - member
    rank = jnp.sum(before * member, axis=1)
    position = owner * capacity + rank
    places = jnp.arange(owners * capacity, dtype=jnp.int32)
    match = position[:, None] == places[None, :]
    filled = jnp.any(match, axis=0)
    source = jnp.sum(
        jnp.where(match, jnp.arange(partial_target_tile.shape[0], dtype=jnp.int32)[:, None], 0),
        axis=0,
    )
    local = jnp.sum(jnp.where(match, (partial_target_tile % chi_dev)[:, None], 0), axis=0)
    slot_ids = jnp.where(filled, local, -1).astype(jnp.float32)
    return (source, filled, slot_ids)


def body(occupied, virtual, cos_weights, pair_occ, pair_virt, partial_target_tile):
    owners = lax.axis_size("tile")
    groups = lax.axis_size("tau")
    part_count = pair_occ.shape[0]
    capacity = 2 * part_count // owners
    chi_dev = CHI_DEV
    tau_count = occupied.shape[0]
    tile_size = occupied.shape[2]
    source, filled, slot_ids = slot_layout(partial_target_tile, chi_dev, owners, capacity)
    mask = filled.astype(jnp.float32)
    rows = tile_size // groups
    partial_value = block_products(occupied, virtual, pair_occ, pair_virt, groups)
    slots = source.shape[0]
    outgoing = jnp.take(partial_value, source, axis=1) * mask[None, :, None, None, None]
    split_rows = outgoing.reshape(groups * slots, tau_count, rows, tile_size)
    repeated_ids = jnp.tile(slot_ids, groups)
    incoming, arrived = (
        lax.all_to_all(split_rows, ("tau", "tile"), split_axis=0, concat_axis=0, tiled=True),
        lax.all_to_all(repeated_ids, ("tau", "tile"), split_axis=0, concat_axis=0, tiled=True),
    )
    incoming = incoming.reshape(groups, slots, tau_count * rows * tile_size)
    arrived = arrived.reshape(groups, slots)
    selector = (
        arrived[:, None, :] == jnp.arange(chi_dev, dtype=jnp.float32)[None, :, None]
    ).astype(jnp.float32)
    chi_time = jnp.einsum("xcs,xsf->cxf", selector, incoming, precision=lax.Precision.HIGHEST)
    chi_time = chi_time.reshape(chi_dev, groups * tau_count, rows, tile_size)
    return jnp.einsum("kt,ctrd->kcrd", cos_weights, chi_time, precision=lax.Precision.HIGHEST)


def solution(mesh):
    in_specs = (
        P("tau", "tile", None, None),
        P("tau", "tile", None, None),
        P(),
        P("tile", None),
        P("tile", None),
        P("tile"),
    )
    out_specs = P(None, "tile", "tau", None)
    return jax.shard_map(body, mesh=mesh, in_specs=in_specs, out_specs=out_specs, check_vma=False)
```

profile of v0, /device:TPU:0, one launch (start us, length us, event | category | flops | bytes accessed | tf_op | source)
XLA Modules:
  0.0 1196.7 jit_solution(1064076904701551448)
XLA Ops:
  2.7 7.3 all-to-all-start.1
  11.7 6.2 broadcast_in_dim.61.clone
  17.9 506.0 %while.13 = (s32[]{:T(128)}, f32[4,192,1,32,128]{4,3,1,0,2:T(8,128)}, bf16[1,128,128,128]{3,2,1,0:T(8,128)(2,1)}, s32[192,16]{1,0:T(8,128)S(1)}, bf16[1,128,128,...) while((s32[]{:T(128)}, ...), condition=%wide.region_5.7_spmd, body=%wide.region_4.6_spmd.sunk | while | flops 541068800 | bytes 35142300 | solution.py:32
  18.0 5.2 gather_fusion
  39.1 5.2 gather_fusion
  60.2 5.2 gather_fusion
  81.2 5.2 gather_fusion
  102.3 5.2 gather_fusion
  123.4 5.2 gather_fusion
  144.5 5.2 gather_fusion
  165.6 5.2 gather_fusion
  186.7 5.2 gather_fusion
  228.9 5.2 gather_fusion
  249.9 5.2 gather_fusion
  334.3 5.2 gather_fusion
  376.4 5.2 gather_fusion
  397.5 5.2 gather_fusion
  523.9 19.4 %gather_fusion.2 = f32[384,4,32,128]{3,2,1,0:T(8,128)} fusion(f32[4,192,32,128]{3,2,1,0:T(8,128)} %bitcast.73, s32[1024]{0:T(1024)S(1)} %pad_clamp_fusion.2), kind=kCustom, calls=%fused_computation.2 | custom fusion | bytes 50333184 | tf_op jit(solution)/shard_map/jit(_take)/gather | solution.py:66
  543.3 17.6 %copy.35 = f32[4,384,32,128]{3,2,1,0:T(8,128)} copy(f32[4,384,32,128]{3,2,0,1:T(8,128)} %bitcast.78) | data formatting | bytes 50331648 | tf_op jit(solution)/shard_map/jit(_take)/gather | solution.py:66
  561.0 21.6 %fusion.9 = f32[1536,1,32,128]{3,2,0,1:T(8,128)} fusion(f32[4,384,32,128]{3,2,1,0:T(8,128)} %copy.35, f32[1536]{0:T(1024)S(1)} %mul.41, pred[1536]{0:T(1024)(128)(4,1)S(1)} %broadcast_in_dim.59), kind=kLoop, calls=%fused_computation.19 | loop fusion | flops 12582912 | bytes 50339328 | tf_op jit(solution)/shard_map/mul | solution.py:66
  582.5 6.0 all-to-all-start
  589.8 559.5 %all-to-all-done = f32[1536,1,32,128]{3,2,1,0:T(8,128)} async-done(((f32[1536,1,32,128]{3,2,1,0:T(8,128)}), f32[1536,1,32,128]{3,2,1,0:T(8,128)}, u32[]{:S(2)}, u32[]{:S(2)}) %all-to-all-start) | async-done | bytes 25165856 | tf_op jit(solution)/shard_map/all_to_all | solution.py:70
  1149.3 27.0 %reshape.99 = f32[4,384,4096]{2,1,0:T(8,128)} reshape(f32[1536,1,32,128]{3,2,1,0:T(8,128)} %all-to-all-done) | data formatting | bytes 50331648 | tf_op jit(solution)/shard_map/reshape | solution.py:73
  1176.3 14.0 %fusion.16 = f32[4,4096,32]{1,2,0:T(8,128)S(1)} fusion(f32[4,384,4096]{2,1,0:T(8,128)} %reshape.99, f32[4,384]{1,0:T(4,128)S(1)} %eq.59), kind=kOutput, calls=%fused_computation.28 | convolution fusion | flops 2415968256 | bytes 27269120 | tf_op jit(solution)/shard_map/xcs,xsf->cxf/dot_general | solution.py:78
  (260 shorter events, 444.2 us)
Async XLA Ops:
  0.0 1190.8 %copy-start = (f32[4,4]{1,0:T(4,128)S(1)}, f32[4,4]{1,0:T(4,128)}, u32[]{:S(2)}) copy-start(f32[4,4]{1,0:T(4,128)} %param.12) | copy-start | bytes 196
  2.7 579.9 %all-to-all-start.1 = ((f32[32,48,1]{1,2,0:T(1,128)}), f32[32,48,1]{1,2,0:T(1,128)S(1)}, u32[]{:S(2)}, u32[]{:S(2)}) async-start(f32[32,48,1]{1,2,0:T(1,128)} %bitcast.18), calls=%async_computation.1 | async-start | bytes 32768 | tf_op jit(solution)/shard_map/all_to_all | solution.py:71
  582.5 566.8 %all-to-all-start = ((f32[1536,1,32,128]{3,2,1,0:T(8,128)}), f32[1536,1,32,128]{3,2,1,0:T(8,128)}, u32[]{:S(2)}, u32[]{:S(2)}) async-start(f32[1536,1,32,128]{3,2,1,0:T(8,128)} %bitcast.79), calls=%async_computation | async-start | bytes 50331648 | tf_op jit(solution)/shard_map/all_to_all | solution.py:70
where the time goes:
time: 1200 us
  waiting for transfers between devices  559 us (47%)
  local copies, waits for them, and re-layouts  351 us (29%)
  matrix products  138 us (12%)
  other arithmetic  134 us (11%)
  starting transfers between devices  13.3 us (1%)
    all_to_all x1, waiting for transfers between devices, body(): lax.all_to_all(split_rows, ('tau', 'tile'), split_axis=0, concat_axis=0,...  559 us
    gather x24, local copies, waits for them, and re-layouts, one_block(): left = jnp.take(occupied[0], occ_rows, axis=0)  126 us
    gather x24, local copies, waits for them, and re-layouts, one_block(): right = jnp.take(virtual[0], virt_rows, axis=0)  126 us
    dot_general x24, matrix products, one_block(): jnp.einsum('bjgrk,bjkc->gbrc', left, right, preferred_element_type=jnp.fl...  120 us
    select_n x24, other arithmetic, one_block(): left = jnp.take(occupied[0], occ_rows, axis=0)  109 us
    gather x2, local copies, waits for them, and re-layouts, body(): jnp.take(partial_value, source, axis=1) * mask[None, :, None, None, None]  37.1 us
    reshape x1, local copies, waits for them, and re-layouts, body(): incoming = incoming.reshape(groups, slots, tau_count * rows * tile_size)  27 us
  transfers between devices with their start and end apart: 2, of which 1 were waited for; matrix products, arithmetic and copies ran while one was open for 48% of the time, Pallas kernels for 0%

commit v1 on v0

v1 whole, which is shorter than its diff:
```python
import functools

import jax
import jax.numpy as jnp
from jax import lax
from jax.experimental import pallas as pl
from jax.experimental.pallas import tpu as pltpu
from jax.sharding import PartitionSpec as P

CHI_DEV = 32
CHUNKS = 4


def products_kernel(first, terms, chi_dev, occ_idx, virt_idx, target, occ, virt, out):
    owners, groups, span, rows, width = out.shape
    count = target.shape[0]

    @pl.loop(0, owners)
    def _(d):
        out[d] = jnp.zeros(out.shape[1:], out.dtype)

    @pl.loop(0, count)
    def _(p):
        tile = target[p]
        owner = tile // chi_dev
        place = tile - owner * chi_dev - first

        @pl.when((place >= 0) & (place < span))
        def _():
            acc = None
            step = 2 if terms % 2 == 0 else 1
            for j in range(0, terms, step):
                base = p * terms + j
                left = [occ[occ_idx[base + i]] for i in range(step)]
                right = [virt[virt_idx[base + i]] for i in range(step)]
                dot = jnp.dot(
                    jnp.concatenate(left, axis=1),
                    jnp.concatenate(right, axis=0),
                    preferred_element_type=jnp.float32,
                )
                acc = dot if acc is None else acc + dot
            for g in range(groups):
                out[owner, g, place] += acc[g * rows : (g + 1) * rows]


def products(occ, virt, occ_idx, virt_idx, target, first, span, owners, groups):
    terms = occ_idx.shape[1]
    size = occ.shape[1]
    smem = pl.BlockSpec(memory_space=pltpu.SMEM)
    vmem = pl.BlockSpec(memory_space=pltpu.VMEM)
    return pl.pallas_call(
        functools.partial(products_kernel, first, terms, CHI_DEV),
        out_shape=jax.ShapeDtypeStruct((owners, groups, span, size // groups, size), jnp.float32),
        in_specs=[smem, smem, smem, vmem, vmem],
        out_specs=vmem,
        compiler_params=pltpu.CompilerParams(vmem_limit_bytes=56 * 1024 * 1024),
        cost_estimate=pl.CostEstimate(
            flops=2 * target.shape[0] * terms * size**3 * span // CHI_DEV,
            bytes_accessed=occ.size * 4 + owners * span * size * size * 4,
            transcendentals=0,
        ),
    )(occ_idx.reshape(-1), virt_idx.reshape(-1), target, occ, virt)


def body(occupied, virtual, cos_weights, pair_occ, pair_virt, partial_target_tile):
    owners = lax.axis_size("tile")
    groups = lax.axis_size("tau")
    span = CHI_DEV // CHUNKS
    results = []
    for q in range(CHUNKS):
        local = products(
            occupied[0], virtual[0], pair_occ, pair_virt, partial_target_tile,
            q * span, span, owners, groups,
        )
        flat = local.reshape((owners * groups * span,) + local.shape[3:])
        owned = lax.psum_scatter(flat, "tile", scatter_dimension=0, tiled=True)
        swapped = lax.all_to_all(owned, "tau", split_axis=0, concat_axis=0, tiled=True)
        by_time = swapped.reshape((groups, span) + local.shape[3:])
        part = sum(cos_weights[:, t, None, None, None] * by_time[t][None] for t in range(groups))
        results.append(part)
    return jnp.concatenate(results, axis=1)


def solution(mesh):
    in_specs = (
        P("tau", "tile", None, None),
        P("tau", "tile", None, None),
        P(),
        P("tile", None),
        P("tile", None),
        P("tile"),
    )
    out_specs = P(None, "tile", "tau", None)
    return jax.shard_map(body, mesh=mesh, in_specs=in_specs, out_specs=out_specs, check_vma=False)
```

time: 1200 us -> 422 us (0.35)
  local copies, waits for them, and re-layouts: 351 us -> 3.37 us
  waiting for transfers between devices: 559 us -> 293 us
  matrix products: 138 us -> 0 us
  other arithmetic: 134 us -> 2.14 us
  Pallas kernels: 0 us -> 94.1 us
  between operations: 0.12 us -> 13.2 us
    all_to_all x2 -> x4, waiting for transfers between devices: 559 us -> 8.54 us  [body(): lax.all_to_all(owned, 'tau', split_axis=0, concat_axis=0, tiled=True)]
    gather x50 -> x0, local copies, waits for them, and re-layouts: 289 us -> none  [the longest x24 126 us: one_block(): left = jnp.take(occupied[0], occ_rows, axis=0)]
    reduce_scatter x0 -> x4, waiting for transfers between devices: none -> 285 us  [body(): owned = lax.psum_scatter(flat, 'tile', scatter_dimension=0, tiled=True)]
    dot_general x26 -> x0, matrix products: 138 us -> none  [the longest x24 120 us: one_block(): jnp.einsum('bjgrk,bjkc->gbrc', left, right, preferred_element_type=jnp.fl...]
    select_n x26 -> x0, other arithmetic: 110 us -> none  [the longest x24 109 us: one_block(): left = jnp.take(occupied[0], occ_rows, axis=0)]
    pallas_call x0 -> x4, Pallas kernels: none -> 94.1 us  [products(): pl.pallas_call(functools.partial(products_kernel, first, terms, CHI_DEV),...]
    reshape x1 -> x2, local copies, waits for them, and re-layouts: 27 us -> 1.38 us  [the longest x1 0.69 us: products(): occ_idx.reshape(-1)]
    mul x1 -> x0, other arithmetic: 21.6 us -> none  [body(): jnp.take(partial_value, source, axis=1) * mask[None, :, None, None, None]]
  transfers between devices with their start and end apart: 2 -> 8, of which waited for: 1 -> 5; matrix products, arithmetic and copies ran while one was open for 48% -> 0% of each run, Pallas kernels for 0% -> 17%
where the time goes in v1:
time: 422 us; the launch traced here: 420 us
  waiting for transfers between devices  293 us (69%)
  Pallas kernels  94.1 us (22%)
  starting transfers between devices  14 us (3%)
  between operations  13.2 us (3%)
    reduce_scatter x4, waiting for transfers between devices, body(): owned = lax.psum_scatter(flat, 'tile', scatter_dimension=0, tiled=True)  285 us
    pallas_call x4, Pallas kernels, products(): pl.pallas_call(functools.partial(products_kernel, first, terms, CHI_DEV),...  94.1 us
    all_to_all x4, starting transfers between devices, body(): lax.all_to_all(owned, 'tau', split_axis=0, concat_axis=0, tiled=True)  13.9 us
    all_to_all x4, waiting for transfers between devices, body(): lax.all_to_all(owned, 'tau', split_axis=0, concat_axis=0, tiled=True)  8.54 us
  transfers between devices with their start and end apart: 8, of which 5 were waited for; matrix products, arithmetic and copies ran while one was open for 0% of the time, Pallas kernels for 17%

profile of v1, /device:TPU:0, one launch (start us, length us, event | category | flops | bytes accessed | tf_op | source)
XLA Modules:
  0.0 420.3 jit_solution(2320465239722945989)
XLA Ops:
  6.5 0.8 copy.7
  7.4 0.7 reshape.64.occ_idx
  8.0 0.8 copy.8
  8.9 0.7 reshape.65.virt_idx
  9.5 23.5 %shard_map.67 = f32[8,4,8,32,128]{4,3,2,1,0:T(8,128)} custom-call(s32[3072]{0:T(1024)} %reshape.64.occ_idx, s32[3072]{0:T(1024)} %reshape.65.virt_idx, s32[192]{0:T(256)} %target.7, bf16[128,128,128]{2,1,0:T(8,128)(2,1)} %bitcast.6, bf16[128,128,128]{2,1,0:T(8,128)(2,1)} %bitcast.10), custom_call_target="tpu_custom_call" | custom-call | flops 3221225472 | bytes 12582912 | tf_op jit(solution)/shard_map/pallas_call | solution.py:51
  33.1 0.0 reduce-scatter.9.cloned.1.call-start
  33.2 24.1 %shard_map.66 = f32[8,4,8,32,128]{4,3,2,1,0:T(8,128)} custom-call(s32[3072]{0:T(1024)} %reshape.64.occ_idx, s32[3072]{0:T(1024)} %reshape.65.virt_idx, s32[192]{0:T(256)} %target.7, bf16[128,128,128]{2,1,0:T(8,128)(2,1)} %bitcast.7, bf16[128,128,128]{2,1,0:T(8,128)(2,1)} %bitcast.11), custom_call_target="tpu_custom_call" | custom-call | flops 3221225472 | bytes 12582912 | tf_op jit(solution)/shard_map/pallas_call | solution.py:51
  57.3 0.0 reduce-scatter.7.cloned.1.call-start
  57.3 24.2 %shard_map.65 = f32[8,4,8,32,128]{4,3,2,1,0:T(8,128)} custom-call(s32[3072]{0:T(1024)} %reshape.64.occ_idx, s32[3072]{0:T(1024)} %reshape.65.virt_idx, s32[192]{0:T(256)} %target.7, bf16[128,128,128]{2,1,0:T(8,128)(2,1)} %bitcast.8, bf16[128,128,128]{2,1,0:T(8,128)(2,1)} %bitcast.12), custom_call_target="tpu_custom_call" | custom-call | flops 3221225472 | bytes 12582912 | tf_op jit(solution)/shard_map/pallas_call | solution.py:51
  81.5 0.0 reduce-scatter.5.cloned.1.call-start
  81.6 22.3 %shard_map.64 = f32[8,4,8,32,128]{4,3,2,1,0:T(8,128)} custom-call(s32[3072]{0:T(1024)} %reshape.64.occ_idx, s32[3072]{0:T(1024)} %reshape.65.virt_idx, s32[192]{0:T(256)} %target.7, bf16[128,128,128]{2,1,0:T(8,128)(2,1)} %bitcast.9, bf16[128,128,128]{2,1,0:T(8,128)(2,1)} %bitcast.13), custom_call_target="tpu_custom_call" | custom-call | flops 3221225472 | bytes 12582912 | tf_op jit(solution)/shard_map/pallas_call | solution.py:51
  103.9 20.9 %reduce-scatter.11.cloned.1.call-done = f32[32,32,128]{2,1,0:T(8,128)} async-done(((f32[256,32,128]{2,1,0:T(8,128)}), f32[32,32,128]{2,1,0:T(8,128)}) %reduce-scatter.11.cloned.1.call-update) | async-done | bytes 524304 | tf_op jit(solution)/shard_map/reduce_scatter | solution.py:76
  124.9 3.5 all-to-all-start.3
  128.3 88.1 %reduce-scatter.9.cloned.1.call-done = f32[32,32,128]{2,1,0:T(8,128)} async-done(((f32[256,32,128]{2,1,0:T(8,128)}), f32[32,32,128]{2,1,0:T(8,128)}) %reduce-scatter.9.cloned.1.call-update) | async-done | bytes 524304 | tf_op jit(solution)/shard_map/reduce_scatter | solution.py:76
  216.5 3.5 all-to-all-start.2
  219.9 0.2 slice_reduce_fusion.3
  220.2 87.9 %reduce-scatter.7.cloned.1.call-done = f32[32,32,128]{2,1,0:T(8,128)} async-done(((f32[256,32,128]{2,1,0:T(8,128)}), f32[32,32,128]{2,1,0:T(8,128)}) %reduce-scatter.7.cloned.1.call-update) | async-done | bytes 524304 | tf_op jit(solution)/shard_map/reduce_scatter | solution.py:76
  308.0 3.5 all-to-all-start.1
  311.6 87.9 %reduce-scatter.5.cloned.1.call-done = f32[32,32,128]{2,1,0:T(8,128)} async-done(((f32[256,32,128]{2,1,0:T(8,128)}), f32[32,32,128]{2,1,0:T(8,128)}) %reduce-scatter.5.cloned.1.call-update) | async-done | bytes 524304 | tf_op jit(solution)/shard_map/reduce_scatter | solution.py:76
  399.5 3.5 all-to-all-start
  403.0 0.2 multiply_add_fusion
  403.2 8.5 %all-to-all-done = f32[32,32,128]{2,1,0:T(8,128)S(1)} async-done(((f32[32,32,128]{2,1,0:T(8,128)}), f32[32,32,128]{2,1,0:T(8,128)S(1)}, u32[]{:S(2)}, u32[]{:S(2)}) %all-to-all-start) | async-done | bytes 524320 | tf_op jit(solution)/shard_map/all_to_all | solution.py:77
  411.8 0.4 multiply_add_fusion.3
  412.2 1.5 pad_maximum_fusion
  (14 shorter events, 0.2 us)
Async XLA Ops:
  6.5 118.3 %reduce-scatter.11.cloned.1.call-start = ((), (), s32[]{:S(2)}) async-start(), calls=%async_computation.11 | async-start | bytes 4718592 | tf_op jit(solution)/shard_map/reduce_scatter | solution.py:76
  33.1 183.3 %reduce-scatter.9.cloned.1.call-start = ((), (), s32[]{:S(2)}) async-start(), calls=%async_computation.10 | async-start | bytes 4718592 | tf_op jit(solution)/shard_map/reduce_scatter | solution.py:76
  57.3 250.7 %reduce-scatter.7.cloned.1.call-start = ((), (), s32[]{:S(2)}) async-start(), calls=%async_computation.9 | async-start | bytes 4718592 | tf_op jit(solution)/shard_map/reduce_scatter | solution.py:76
  81.5 318.0 %reduce-scatter.5.cloned.1.call-start = ((), (), s32[]{:S(2)}) async-start(), calls=%async_computation.8 | async-start | bytes 4718592 | tf_op jit(solution)/shard_map/reduce_scatter | solution.py:76
  103.9 116.0 %copy-start = (f32[4,4]{1,0:T(4,128)S(1)}, f32[4,4]{1,0:T(4,128)}, u32[]{:S(2)}) copy-start(f32[4,4]{1,0:T(4,128)} %param.8) | copy-start | bytes 196
  124.9 91.6 %all-to-all-start.3 = ((f32[32,32,128]{2,1,0:T(8,128)}), f32[32,32,128]{2,1,0:T(8,128)S(1)}, u32[]{:S(2)}, u32[]{:S(2)}) async-start(f32[32,32,128]{2,1,0:T(8,128)} %reduce-scatter.11.cloned.1.call-done), calls=%async_computation.7 | async-start | bytes 1048576 | tf_op jit(solution)/shard_map/all_to_all | solution.py:77
  216.5 91.6 %all-to-all-start.2 = ((f32[32,32,128]{2,1,0:T(8,128)}), f32[32,32,128]{2,1,0:T(8,128)S(1)}, u32[]{:S(2)}, u32[]{:S(2)}) async-start(f32[32,32,128]{2,1,0:T(8,128)} %reduce-scatter.9.cloned.1.call-done), calls=%async_computation.5 | async-start | bytes 1048576 | tf_op jit(solution)/shard_map/all_to_all | solution.py:77
  308.0 91.4 %all-to-all-start.1 = ((f32[32,32,128]{2,1,0:T(8,128)}), f32[32,32,128]{2,1,0:T(8,128)S(1)}, u32[]{:S(2)}, u32[]{:S(2)}) async-start(f32[32,32,128]{2,1,0:T(8,128)} %reduce-scatter.7.cloned.1.call-done), calls=%async_computation.3 | async-start | bytes 1048576 | tf_op jit(solution)/shard_map/all_to_all | solution.py:77
  399.5 12.3 %all-to-all-start = ((f32[32,32,128]{2,1,0:T(8,128)}), f32[32,32,128]{2,1,0:T(8,128)S(1)}, u32[]{:S(2)}, u32[]{:S(2)}) async-start(f32[32,32,128]{2,1,0:T(8,128)} %reduce-scatter.5.cloned.1.call-done), calls=%async_computation.1 | async-start | bytes 1048576 | tf_op jit(solution)/shard_map/all_to_all | solution.py:77
Sparse Core Ops, SparseCore 0:
  33.2 91.5 reduce-scatter.10
  128.5 87.9 reduce-scatter.8
  220.1 87.8 reduce-scatter.6
  311.5 87.9 reduce-scatter.4

commit v2 on v1

v2 whole, which is shorter than its diff:
```python
import functools

import jax
import jax.numpy as jnp
from jax import lax
from jax.experimental import pallas as pl
from jax.experimental.pallas import tpu as pltpu
from jax.sharding import PartitionSpec as P

CHI_DEV = 32
UNIT = 4
BUDGET = 46 * 1024 * 1024
MESH = pl.DeviceIdType.MESH


def products_kernel(first, terms, chi_dev, occ_idx, virt_idx, target, occ, virt, out):
    owners, units, groups, each, rows, width = out.shape
    span = units * each
    count = target.shape[0]

    @pl.loop(0, owners)
    def _(d):
        out[d] = jnp.zeros(out.shape[1:], out.dtype)

    @pl.loop(0, count)
    def _(p):
        tile = target[p]
        owner = tile // chi_dev
        place = tile - owner * chi_dev - first

        @pl.when((place >= 0) & (place < span))
        def _():
            unit = place // each
            acc = None
            step = 2 if terms % 2 == 0 else 1
            for j in range(0, terms, step):
                base = p * terms + j
                left = [occ[occ_idx[base + i]] for i in range(step)]
                right = [virt[virt_idx[base + i]] for i in range(step)]
                dot = jnp.dot(
                    jnp.concatenate(left, axis=1),
                    jnp.concatenate(right, axis=0),
                    preferred_element_type=jnp.float32,
                )
                acc = dot if acc is None else acc + dot
            for g in range(groups):
                out[owner, unit, g, place - unit * each] += acc[g * rows : (g + 1) * rows]


def products(occ, virt, occ_idx, virt_idx, target, first, span, each, owners, groups):
    terms = occ_idx.shape[1]
    size = occ.shape[1]
    smem = pl.BlockSpec(memory_space=pltpu.SMEM)
    vmem = pl.BlockSpec(memory_space=pltpu.VMEM)
    return pl.pallas_call(
        functools.partial(products_kernel, first, terms, CHI_DEV),
        out_shape=jax.ShapeDtypeStruct(
            (owners, span // each, groups, each, size // groups, size), jnp.float32
        ),
        in_specs=[smem, smem, smem, vmem, vmem],
        out_specs=vmem,
        compiler_params=pltpu.CompilerParams(vmem_limit_bytes=56 * 1024 * 1024),
        cost_estimate=pl.CostEstimate(
            flops=2 * target.shape[0] * terms * size**3 * span // CHI_DEV,
            bytes_accessed=occ.size * 4 + owners * span * size * size * 4,
            transcendentals=0,
        ),
    )(occ_idx.reshape(-1), virt_idx.reshape(-1), target, occ, virt)


def line_slots(n):
    if n == 1:
        return 0
    return 1 if n == 2 else 2 * (n - 1)


class Line:
    def __init__(self, n, place, device, own, slots, send_sem, recv_sem, hold=None):
        self.hold = hold
        self.n, self.place, self.device = n, place, device
        self.own, self.slots, self.send_sem, self.recv_sem = own, slots, send_sem, recv_sem

    def slot(self, right, d):
        if right:
            return d - 1
        return d if self.n == 2 else self.n - 1 + d

    def copy(self, right, u, d, src, back=False):
        s = self.slot(right, d)
        k = u * line_slots(self.n) + s
        return pltpu.make_async_remote_copy(
            src_ref=src,
            dst_ref=self.slots.at[s, u],
            send_sem=self.send_sem.at[k],
            recv_sem=self.recv_sem.at[k],
            device_id={"tile": self.device(1 if right != back else -1)},
            device_id_type=MESH,
        )

    def routes(self):
        for right in (True, False):
            for d in range(self.n - 1, 0, -1) if right else range(self.n - 1):
                yield right, d

    def launch(self, u):
        for right, d in self.routes():
            @pl.when(self.place == (0 if right else self.n - 1))
            def _():
                self.copy(right, u, d, self.own(d, u)).start()

    def merge(self, u):
        if self.n == 2:
            return
        for right, d in self.routes():
            inner = (self.place > 0) & (self.place < d) if right else (
                (self.place < self.n - 1) & (self.place > d))

            @pl.when(inner)
            def _():
                here = self.slots.at[self.slot(right, d), u]
                copy = self.copy(right, u, d, here)
                copy.wait_recv()
                own = self.own(d, u)
                if self.hold is not None:
                    buffer, sem = self.hold
                    fetch = pltpu.make_async_copy(own, buffer, sem)
                    fetch.start()
                    fetch.wait()
                    own = buffer
                here[...] += own[...]
                copy.start()

    def final(self, u, into):
        for right in (True, False):
            @pl.when(self.place > 0 if right else self.place < self.n - 1)
            def _():
                k = self.slot(right, self.place)
                here = self.slots.at[k, u]
                self.copy(right, u, self.place, here, back=True).wait_recv()
                into[...] += here[...]

    def drain(self, u):
        for right, d in self.routes():
            @pl.when(self.place < d if right else self.place > d)
            def _():
                self.copy(right, u, d, self.slots.at[self.slot(right, d), u]).wait_send()


def scatter_kernel(ny, nz, groups, weights, dense, out, mine, y_slots, z_slots, times,
                   load_sem, y_send, y_recv, z_send, z_recv, t_send, t_recv, hold, hold_sem):
    tau = lax.axis_index("tau")
    tile = lax.axis_index("tile")
    z, y = tile // ny, tile % ny
    units = mine.shape[0]
    each = mine.shape[3]
    freqs = out.shape[0]

    y_line = Line(ny, y, lambda step: tile + step, lambda d, u: dense.at[:, d, u],
                  y_slots, y_send, y_recv, (hold, hold_sem))
    z_line = Line(nz, z, lambda step: tile + step * ny, lambda d, u: mine.at[u, d],
                  z_slots, z_send, z_recv)

    barrier = pltpu.get_barrier_semaphore()
    for step in range(1, groups):
        pl.semaphore_signal(barrier, inc=1, device_id={"tau": (tau + step) % groups},
                            device_id_type=MESH)
    for step in range(1, ny):
        pl.semaphore_signal(barrier, inc=1, device_id={"tile": z * ny + (y + step) % ny},
                            device_id_type=MESH)
    for step in range(1, nz):
        pl.semaphore_signal(barrier, inc=1, device_id={"tile": (z + step) % nz * ny + y},
                            device_id_type=MESH)
    pl.semaphore_wait(barrier, groups - 1 + ny - 1 + nz - 1)

    def load(u):
        return pltpu.make_async_copy(dense.at[:, y, u], mine.at[u], load_sem.at[u])

    def swap(u, step):
        other = (tau + step) % groups
        return pltpu.make_async_remote_copy(
            src_ref=mine.at[u, z, other],
            dst_ref=times.at[u, tau],
            send_sem=t_send.at[u * groups + step],
            recv_sem=t_recv.at[u * groups + tau],
            device_id={"tau": other},
            device_id_type=MESH,
        )

    def arrived(u, source):
        return pltpu.make_async_remote_copy(
            src_ref=mine.at[u, z, 0],
            dst_ref=times.at[u, source],
            send_sem=t_send.at[u * groups],
            recv_sem=t_recv.at[u * groups + source],
            device_id={"tau": source},
            device_id_type=MESH,
        )

    @pl.loop(0, units)
    def _(u):
        y_line.launch(u)
        load(u).start()

    @pl.loop(0, units + 2)
    def _(t):
        @pl.when(t < units)
        def _():
            load(t).wait()
            y_line.merge(t)
            y_line.final(t, mine.at[t])
            z_line.launch(t)

        @pl.when((t >= 1) & (t < units + 1))
        def _():
            u = t - 1
            z_line.merge(u)
            z_line.final(u, mine.at[u, z])
            for step in range(1, groups):
                swap(u, step).start()
            times[u, tau] = mine[u, z, tau]

        @pl.when(t >= 2)
        def _():
            u = t - 2
            for step in range(1, groups):
                arrived(u, (tau + step) % groups).wait_recv()
            for e in range(each):
                for k in range(freqs):
                    total = weights[k, 0] * times[u, 0, e]
                    for s in range(1, groups):
                        total += weights[k, s] * times[u, s, e]
                    out[k, u * each + e] = total

    @pl.loop(0, units)
    def _(u):
        y_line.drain(u)
        z_line.drain(u)
        for step in range(1, groups):
            swap(u, step).wait_send()


def scatter(dense, weights, ny, nz, groups):
    owners, units, _, each, rows, width = dense.shape
    freqs = weights.shape[0]
    block = (groups, each, rows, width)
    ys, zs = max(line_slots(ny), 1), max(line_slots(nz), 1)
    dma = pltpu.SemaphoreType.DMA
    return pl.pallas_call(
        functools.partial(scatter_kernel, ny, nz, groups),
        out_shape=jax.ShapeDtypeStruct((freqs, units * each, rows, width), jnp.float32),
        in_specs=[pl.BlockSpec(memory_space=pltpu.SMEM), pl.BlockSpec(memory_space=pl.ANY)],
        out_specs=pl.BlockSpec(memory_space=pltpu.VMEM),
        scratch_shapes=[
            pltpu.VMEM((units, nz) + block, jnp.float32),
            pltpu.VMEM((ys, units, nz) + block, jnp.float32),
            pltpu.VMEM((zs, units) + block, jnp.float32),
            pltpu.VMEM((units, groups, each, rows, width), jnp.float32),
            dma((units,)),
            dma((units * ys,)),
            dma((units * ys,)),
            dma((units * zs,)),
            dma((units * zs,)),
            dma((units * groups,)),
            dma((units * groups,)),
            pltpu.VMEM((nz,) + block if ny > 2 else (8, 128), jnp.float32),
            dma,
        ],
        compiler_params=pltpu.CompilerParams(
            collective_id=0, has_side_effects=True, vmem_limit_bytes=58 * 1024 * 1024),
    )(weights, dense.reshape((nz, ny) + dense.shape[1:]))


def body(occupied, virtual, cos_weights, pair_occ, pair_virt, partial_target_tile):
    owners = lax.axis_size("tile")
    groups = lax.axis_size("tau")
    size = occupied.shape[2]
    ny = 1
    while 2 * ny * 2 * ny <= owners:
        ny *= 2
    nz = owners // ny
    tile_bytes = 4 * size * size
    span = CHI_DEV
    while span > UNIT and span * tile_bytes * (
        nz * (1 + line_slots(ny)) + line_slots(nz) + 2
    ) > BUDGET:
        span //= 2
    results = []
    for q in range(CHI_DEV // span):
        dense = products(
            occupied[0], virtual[0], pair_occ, pair_virt, partial_target_tile,
            q * span, span, min(UNIT, span), owners, groups,
        )
        results.append(scatter(dense, cos_weights, ny, nz, groups))
    return results[0] if len(results) == 1 else jnp.concatenate(results, axis=1)


def solution(mesh):
    in_specs = (
        P("tau", "tile", None, None),
        P("tau", "tile", None, None),
        P(),
        P("tile", None),
        P("tile", None),
        P("tile"),
    )
    out_specs = P(None, "tile", "tau", None)
    return jax.shard_map(body, mesh=mesh, in_specs=in_specs, out_specs=out_specs, check_vma=False)
```

time: 422 us -> 305 us (0.72)
  waiting for transfers between devices: 293 us -> 0 us
  Pallas kernels: 94.1 us -> 299 us
  starting transfers between devices: 14 us -> 0 us
  between operations: 13.2 us -> 0.01 us
    reduce_scatter x4 -> x0, waiting for transfers between devices: 285 us -> none  [body(): owned = lax.psum_scatter(flat, 'tile', scatter_dimension=0, tiled=True)]
    pallas_call x0 -> x1, Pallas kernels: none -> 230 us  [scatter(): pl.pallas_call(functools.partial(scatter_kernel, ny, nz, groups), out_sha...]
    pallas_call x4 -> x1, Pallas kernels: 94.1 us -> 68.8 us  [products(): pl.pallas_call(functools.partial(products_kernel, first, terms, CHI_DEV),...]
    all_to_all x4 -> x0, starting transfers between devices: 13.9 us -> none  [body(): lax.all_to_all(owned, 'tau', split_axis=0, concat_axis=0, tiled=True)]
    all_to_all x4 -> x0, waiting for transfers between devices: 8.54 us -> none  [body(): lax.all_to_all(owned, 'tau', split_axis=0, concat_axis=0, tiled=True)]
  transfers between devices with their start and end apart: 8 -> 0, of which waited for: 5 -> 0; matrix products, arithmetic and copies ran while one was open for 0% -> 0% of each run, Pallas kernels for 17% -> 0%
where the time goes in v2:
time: 305 us
  Pallas kernels  299 us (98%)
  local copies, waits for them, and re-layouts  6.09 us (2%)
    pallas_call x1, Pallas kernels, scatter(): pl.pallas_call(functools.partial(scatter_kernel, ny, nz, groups), out_sha...  230 us
    pallas_call x1, Pallas kernels, products(): pl.pallas_call(functools.partial(products_kernel, first, terms, CHI_DEV),...  68.8 us

profile of v2, /device:TPU:0, one launch (start us, length us, event | category | flops | bytes accessed | tf_op | source)
XLA Modules:
  0.0 304.8 jit_solution(15555805414569389149)
XLA Ops:
  0.0 0.8 copy.7
  0.8 0.7 reshape.9.occ_idx
  1.5 0.8 copy.8
  2.3 0.7 reshape.10.virt_idx
  3.0 68.8 %shard_map.64 = f32[8,8,4,4,32,128]{5,4,3,2,1,0:T(8,128)} custom-call(s32[3072]{0:T(1024)} %reshape.9.occ_idx, s32[3072]{0:T(1024)} %reshape.10.virt_idx, s32[192]{0:T(256)} %target.1, bf16[128,128,128]{2,1,0:T(8,128)(2,1)} %bitcast.4, bf16[128,128,128]{2,1,0:T(8,128)(2,1)} %bitcast.5), custom_call_target="tpu_custom_call" | custom-call | flops 12884901888 | bytes 25165824 | tf_op jit(solution)/shard_map/pallas_call | solution.py:55
  71.8 230.0 %shard_map.65 = f32[4,32,32,128]{3,2,1,0:T(8,128)} custom-call(f32[4,4]{1,0:T(4,128)} %weights.1, f32[4,2,8,4,4,32,128]{6,5,4,3,2,1,0:T(8,128)} %bitcast.3), custom_call_target="tpu_custom_call" | custom-call | tf_op jit(solution)/shard_map/pallas_call | solution.py:248
  301.7 3.1 %copy.10 = f32[4,32,32,128]{3,2,1,0:T(8,128)} copy(f32[4,32,32,128]{3,2,1,0:T(8,128)} %shard_map.65) | data formatting | bytes 4194304

commit v3 on v2

--- a/solution.py
+++ b/solution.py
@@ -1,4 +1,5 @@
 import functools
+import math
 
 import jax
 import jax.numpy as jnp
@@ -22,29 +23,30 @@
     def _(d):
         out[d] = jnp.zeros(out.shape[1:], out.dtype)
 
-    @pl.loop(0, count)
+    unroll = math.gcd(count, 4) if span == chi_dev else 1
+
+    @pl.loop(0, count, unroll=unroll)
     def _(p):
         tile = target[p]
         owner = tile // chi_dev
         place = tile - owner * chi_dev - first
 
-        @pl.when((place >= 0) & (place < span))
-        def _():
+        def add():
             unit = place // each
-            acc = None
-            step = 2 if terms % 2 == 0 else 1
-            for j in range(0, terms, step):
-                base = p * terms + j
-                left = [occ[occ_idx[base + i]] for i in range(step)]
-                right = [virt[virt_idx[base + i]] for i in range(step)]
-                dot = jnp.dot(
-                    jnp.concatenate(left, axis=1),
-                    jnp.concatenate(right, axis=0),
-                    preferred_element_type=jnp.float32,
-                )
-                acc = dot if acc is None else acc + dot
+            left = [occ[occ_idx[p * terms + j]] for j in range(terms)]
+            right = [virt[virt_idx[p * terms + j]] for j in range(terms)]
+            acc = jnp.dot(
+                jnp.concatenate(left, axis=1),
+                jnp.concatenate(right, axis=0),
+                preferred_element_type=jnp.float32,
+            )
             for g in range(groups):
                 out[owner, unit, g, place - unit * each] += acc[g * rows : (g + 1) * rows]
+
+        if span == chi_dev:
+            add()
+        else:
+            pl.when((place >= 0) & (place < span))(add)
 
 
 def products(occ, virt, occ_idx, virt_idx, target, first, span, each, owners, groups):
@@ -147,11 +149,13 @@
 
 
 def scatter_kernel(ny, nz, groups, weights, dense, out, mine, y_slots, z_slots, times,
-                   load_sem, y_send, y_recv, z_send, z_recv, t_send, t_recv, hold, hold_sem):
+                   load_sem, y_send, y_recv, z_send, z_recv, t_send, t_recv, hold, hold_sem,
+                   both, z2_slots, y2_slots, both_sem, z2_send, z2_recv, y2_send, y2_recv):
     tau = lax.axis_index("tau")
     tile = lax.axis_index("tile")
     z, y = tile // ny, tile % ny
     units = mine.shape[0]
+    last = units - 1
     each = mine.shape[3]
     freqs = out.shape[0]
 
@@ -159,6 +163,9 @@
                   y_slots, y_send, y_recv, (hold, hold_sem))
     z_line = Line(nz, z, lambda step: tile + step * ny, lambda d, u: mine.at[u, d],
                   z_slots, z_send, z_recv)
+
+    z2_line = Line(nz, z, z_line.device, lambda d, u: both.at[d], z2_slots, z2_send, z2_recv)
+    y2_line = Line(ny, y, y_line.device, lambda d, u: both.at[z, d], y2_slots, y2_send, y2_recv)
 
     barrier = pltpu.get_barrier_semaphore()
     for step in range(1, groups):
@@ -196,25 +203,47 @@
             device_id_type=MESH,
         )
 
-    @pl.loop(0, units)
+    whole = pltpu.make_async_copy(dense.at[:, :, last], both, both_sem)
+    whole.start()
+
+    @pl.loop(0, last)
     def _(u):
         y_line.launch(u)
         load(u).start()
 
+    whole.wait()
+    z2_line.launch(0)
+    z2_line.merge(0)
+
     @pl.loop(0, units + 2)
     def _(t):
-        @pl.when(t < units)
+        @pl.when(t < last)
         def _():
             load(t).wait()
             y_line.merge(t)
             y_line.final(t, mine.at[t])
             z_line.launch(t)
 
-        @pl.when((t >= 1) & (t < units + 1))
+        @pl.when(t == 0)
+        def _():
+            z2_line.final(0, both.at[z])
+            y2_line.launch(0)
+
+        @pl.when((t >= 1) & (t < units))
         def _():
             u = t - 1
             z_line.merge(u)
             z_line.final(u, mine.at[u, z])
+
+        @pl.when(t == units)
+        def _():
+            y2_line.merge(0)
+            mine[last, z] = both[z, y]
+            y2_line.final(0, mine.at[last, z])
+
+        @pl.when((t >= 1) & (t < units + 1))
+        def _():
+            u = t - 1
             for step in range(1, groups):
                 swap(u, step).start()
             times[u, tau] = mine[u, z, tau]
@@ -231,10 +260,16 @@
                         total += weights[k, s] * times[u, s, e]
                     out[k, u * each + e] = total
 
-    @pl.loop(0, units)
+    z2_line.drain(0)
+    y2_line.drain(0)
+
+    @pl.loop(0, last)
     def _(u):
         y_line.drain(u)
         z_line.drain(u)
+
+    @pl.loop(0, units)
+    def _(u):
         for step in range(1, groups):
             swap(u, step).wait_send()
 
@@ -264,6 +299,14 @@
             dma((units * groups,)),
             pltpu.VMEM((nz,) + block if ny > 2 else (8, 128), jnp.float32),
             dma,
+            pltpu.VMEM((nz, ny) + block, jnp.float32),
+            pltpu.VMEM((zs, 1, ny) + block, jnp.float32),
+            pltpu.VMEM((ys, 1) + block, jnp.float32),
+            dma,
+            dma((zs,)),
+            dma((zs,)),
+            dma((ys,)),
+            dma((ys,)),
         ],
         compiler_params=pltpu.CompilerParams(
             collective_id=0, has_side_effects=True, vmem_limit_bytes=58 * 1024 * 1024),

time: 305 us -> 258 us (0.85)
  Pallas kernels: 299 us -> 252 us
    pallas_call x1, Pallas kernels: 68.8 us -> 44.2 us  [products(): pl.pallas_call(functools.partial(products_kernel, first, terms, CHI_DEV),...]
    pallas_call x1, Pallas kernels: 230 us -> 207 us  [scatter(): pl.pallas_call(functools.partial(scatter_kernel, ny, nz, groups), out_sha...]
where the time goes in v3:
time: 258 us
  Pallas kernels  252 us (98%)
  local copies, waits for them, and re-layouts  6.09 us (2%)
    pallas_call x1, Pallas kernels, scatter(): pl.pallas_call(functools.partial(scatter_kernel, ny, nz, groups), out_sha...  207 us
    pallas_call x1, Pallas kernels, products(): pl.pallas_call(functools.partial(products_kernel, first, terms, CHI_DEV),...  44.2 us

profile of v3, /device:TPU:0, one launch (start us, length us, event | category | flops | bytes accessed | tf_op | source)
XLA Modules:
  0.0 257.8 jit_solution(3954660887108697895)
XLA Ops:
  0.0 0.8 copy.7
  0.8 0.7 reshape.9.occ_idx
  1.5 0.8 copy.8
  2.3 0.7 reshape.10.virt_idx
  3.0 44.2 %shard_map.64 = f32[8,8,4,4,32,128]{5,4,3,2,1,0:T(8,128)} custom-call(s32[3072]{0:T(1024)} %reshape.9.occ_idx, s32[3072]{0:T(1024)} %reshape.10.virt_idx, s32[192]{0:T(256)} %target.1, bf16[128,128,128]{2,1,0:T(8,128)(2,1)} %bitcast.4, bf16[128,128,128]{2,1,0:T(8,128)(2,1)} %bitcast.5), custom_call_target="tpu_custom_call" | custom-call | flops 12884901888 | bytes 25165824 | tf_op jit(solution)/shard_map/pallas_call | solution.py:57
  47.3 207.5 %shard_map.65 = f32[4,32,32,128]{3,2,1,0:T(8,128)} custom-call(f32[4,4]{1,0:T(4,128)} %weights.1, f32[4,2,8,4,4,32,128]{6,5,4,3,2,1,0:T(8,128)} %bitcast.3), custom_call_target="tpu_custom_call" | custom-call | tf_op jit(solution)/shard_map/pallas_call | solution.py:283
  254.7 3.1 %copy.10 = f32[4,32,32,128]{3,2,1,0:T(8,128)} copy(f32[4,32,32,128]{3,2,1,0:T(8,128)} %shard_map.65) | data formatting | bytes 4194304

commit v4 on v3

--- a/solution.py
+++ b/solution.py
@@ -9,7 +9,8 @@
 from jax.sharding import PartitionSpec as P
 
 CHI_DEV = 32
-UNIT = 4
+UNIT = 2
+Z_FIRST = 3 / 16
 BUDGET = 46 * 1024 * 1024
 MESH = pl.DeviceIdType.MESH
 
@@ -33,8 +34,8 @@
 
         def add():
             unit = place // each
-            left = [occ[occ_idx[p * terms + j]] for j in range(terms)]
-            right = [virt[virt_idx[p * terms + j]] for j in range(terms)]
+            left = [occ[occ_idx[j, p]] for j in range(terms)]
+            right = [virt[virt_idx[j, p]] for j in range(terms)]
             acc = jnp.dot(
                 jnp.concatenate(left, axis=1),
                 jnp.concatenate(right, axis=0),
@@ -67,7 +68,7 @@
             bytes_accessed=occ.size * 4 + owners * span * size * size * 4,
             transcendentals=0,
         ),
-    )(occ_idx.reshape(-1), virt_idx.reshape(-1), target, occ, virt)
+    )(occ_idx.T, virt_idx.T, target, occ, virt)
 
 
 def line_slots(n):
@@ -155,7 +156,8 @@
     tile = lax.axis_index("tile")
     z, y = tile // ny, tile % ny
     units = mine.shape[0]
-    last = units - 1
+    lead = both.shape[0]
+    last = units - lead
     each = mine.shape[3]
     freqs = out.shape[0]
 
@@ -164,8 +166,8 @@
     z_line = Line(nz, z, lambda step: tile + step * ny, lambda d, u: mine.at[u, d],
                   z_slots, z_send, z_recv)
 
-    z2_line = Line(nz, z, z_line.device, lambda d, u: both.at[d], z2_slots, z2_send, z2_recv)
-    y2_line = Line(ny, y, y_line.device, lambda d, u: both.at[z, d], y2_slots, y2_send, y2_recv)
+    z2_line = Line(nz, z, z_line.device, lambda d, u: both.at[u, d], z2_slots, z2_send, z2_recv)
+    y2_line = Line(ny, y, y_line.device, lambda d, u: both.at[u, z, d], y2_slots, y2_send, y2_recv)
 
     barrier = pltpu.get_barrier_semaphore()
     for step in range(1, groups):
@@ -203,17 +205,26 @@
             device_id_type=MESH,
         )
 
-    whole = pltpu.make_async_copy(dense.at[:, :, last], both, both_sem)
-    whole.start()
+    def whole(w):
+        return pltpu.make_async_copy(dense.at[:, :, last + w], both.at[w], both_sem.at[w])
+
+    @pl.loop(0, lead)
+    def _(w):
+        whole(w).start()
 
     @pl.loop(0, last)
     def _(u):
         y_line.launch(u)
         load(u).start()
 
-    whole.wait()
-    z2_line.launch(0)
-    z2_line.merge(0)
+    @pl.loop(0, lead)
+    def _(w):
+        whole(w).wait()
+        z2_line.launch(w)
+
+    @pl.loop(0, lead)
+    def _(w):
+        z2_line.merge(w)
 
     @pl.loop(0, units + 2)
     def _(t):
@@ -224,22 +235,23 @@
             y_line.final(t, mine.at[t])
             z_line.launch(t)
 
-        @pl.when(t == 0)
-        def _():
-            z2_line.final(0, both.at[z])
-            y2_line.launch(0)
-
-        @pl.when((t >= 1) & (t < units))
+        @pl.when(t < lead)
+        def _():
+            z2_line.final(t, both.at[t, z])
+            y2_line.launch(t)
+
+        @pl.when((t >= 1) & (t < last + 1))
         def _():
             u = t - 1
             z_line.merge(u)
             z_line.final(u, mine.at[u, z])
 
-        @pl.when(t == units)
-        def _():
-            y2_line.merge(0)
-            mine[last, z] = both[z, y]
-            y2_line.final(0, mine.at[last, z])
+        @pl.when((t >= last + 1) & (t < units + 1))
+        def _():
+            w = t - 1 - last
+            y2_line.merge(w)
+            mine[t - 1, z] = both[w, z, y]
+            y2_line.final(w, mine.at[t - 1, z])
 
         @pl.when((t >= 1) & (t < units + 1))
         def _():
@@ -260,8 +272,10 @@
                         total += weights[k, s] * times[u, s, e]
                     out[k, u * each + e] = total
 
-    z2_line.drain(0)
-    y2_line.drain(0)
+    @pl.loop(0, lead)
+    def _(w):
+        z2_line.drain(w)
+        y2_line.drain(w)
 
     @pl.loop(0, last)
     def _(u):
@@ -278,6 +292,7 @@
     owners, units, _, each, rows, width = dense.shape
     freqs = weights.shape[0]
     block = (groups, each, rows, width)
+    lead = max(1, int(units * Z_FIRST))
     ys, zs = max(line_slots(ny), 1), max(line_slots(nz), 1)
     dma = pltpu.SemaphoreType.DMA
     return pl.pallas_call(
@@ -299,14 +314,14 @@
             dma((units * groups,)),
             pltpu.VMEM((nz,) + block if ny > 2 else (8, 128), jnp.float32),
             dma,
-            pltpu.VMEM((nz, ny) + block, jnp.float32),
-            pltpu.VMEM((zs, 1, ny) + block, jnp.float32),
-            pltpu.VMEM((ys, 1) + block, jnp.float32),
-            dma,
-            dma((zs,)),
-            dma((zs,)),
-            dma((ys,)),
-            dma((ys,)),
+            pltpu.VMEM((lead, nz, ny) + block, jnp.float32),
+            pltpu.VMEM((zs, lead, ny) + block, jnp.float32),
+            pltpu.VMEM((ys, lead) + block, jnp.float32),
+            dma((lead,)),
+            dma((lead * zs,)),
+            dma((lead * zs,)),
+            dma((lead * ys,)),
+            dma((lead * ys,)),
         ],
         compiler_params=pltpu.CompilerParams(
             collective_id=0, has_side_effects=True, vmem_limit_bytes=58 * 1024 * 1024),

time: 258 us -> 258 us (level)
  local copies, waits for them, and re-layouts: 6.09 us -> 3.08 us
  Pallas kernels: 252 us -> 255 us
    pallas_call x1, Pallas kernels: 207 us -> 211 us  [scatter(): pl.pallas_call(functools.partial(scatter_kernel, ny, nz, groups), out_sha...]
where the time goes in v4:
time: 258 us
  Pallas kernels  255 us (99%)
  local copies, waits for them, and re-layouts  3.08 us (1%)
    pallas_call x1, Pallas kernels, scatter(): pl.pallas_call(functools.partial(scatter_kernel, ny, nz, groups), out_sha...  211 us
    pallas_call x1, Pallas kernels, products(): pl.pallas_call(functools.partial(products_kernel, first, terms, CHI_DEV),...  44.2 us

profile of v4, /device:TPU:0, one launch (start us, length us, event | category | flops | bytes accessed | tf_op | source)
XLA Modules:
  0.0 257.9 jit_solution(5460998020692210545)
XLA Ops:
  0.0 44.2 %shard_map.64 = f32[8,16,4,2,32,128]{5,4,3,2,1,0:T(8,128)} custom-call(s32[16,192]{1,0:T(8,128)} %bitcast.8, s32[16,192]{1,0:T(8,128)} %bitcast.9, s32[192]{0:T(256)} %target.1, bf16[128,128,128]{2,1,0:T(8,128)(2,1)} %bitcast.6, bf16[128,128,128]{2,1,0:T(8,128)(2,1)} %bitcast.7), custom_call_target="tpu_custom_call" | custom-call | flops 12884901888 | bytes 25165824 | tf_op jit(solution)/shard_map/pallas_call | solution.py:58
  44.2 210.6 %shard_map.65 = f32[4,32,32,128]{3,2,1,0:T(8,128)} custom-call(f32[4,4]{1,0:T(4,128)} %weights.1, f32[4,2,16,4,2,32,128]{6,5,4,3,2,1,0:T(8,128)} %bitcast.5), custom_call_target="tpu_custom_call" | custom-call | tf_op jit(solution)/shard_map/pallas_call | solution.py:298
  254.9 3.1 %copy.8 = f32[4,32,32,128]{3,2,1,0:T(8,128)} copy(f32[4,32,32,128]{3,2,1,0:T(8,128)} %shard_map.65) | data formatting | bytes 4194304

commit v5 on v4

--- a/solution.py
+++ b/solution.py
@@ -10,6 +10,7 @@
 
 CHI_DEV = 32
 UNIT = 2
+WINDOW = 3
 Z_FIRST = 3 / 16
 BUDGET = 46 * 1024 * 1024
 MESH = pl.DeviceIdType.MESH
@@ -214,7 +215,10 @@
 
     @pl.loop(0, last)
     def _(u):
-        y_line.launch(u)
+        @pl.when(u < WINDOW)
+        def _():
+            y_line.launch(u)
+
         load(u).start()
 
     @pl.loop(0, lead)
@@ -233,6 +237,11 @@
             load(t).wait()
             y_line.merge(t)
             y_line.final(t, mine.at[t])
+
+            @pl.when(t + WINDOW < last)
+            def _():
+                y_line.launch(t + WINDOW)
+
             z_line.launch(t)
 
         @pl.when(t < lead)

time: 258 us -> 282 us (1.093)
  Pallas kernels: 255 us -> 279 us
    pallas_call x1, Pallas kernels: 211 us -> 235 us  [scatter(): pl.pallas_call(functools.partial(scatter_kernel, ny, nz, groups), out_sha...]
where the time goes in v5:
time: 282 us
  Pallas kernels  279 us (99%)
  local copies, waits for them, and re-layouts  3.08 us (1%)
    pallas_call x1, Pallas kernels, scatter(): pl.pallas_call(functools.partial(scatter_kernel, ny, nz, groups), out_sha...  235 us
    pallas_call x1, Pallas kernels, products(): pl.pallas_call(functools.partial(products_kernel, first, terms, CHI_DEV),...  44.2 us

profile of v5, /device:TPU:0, one launch (start us, length us, event | category | flops | bytes accessed | tf_op | source)
XLA Modules:
  0.0 282.1 jit_solution(8580349327217603179)
XLA Ops:
  0.0 44.2 %shard_map.64 = f32[8,16,4,2,32,128]{5,4,3,2,1,0:T(8,128)} custom-call(s32[16,192]{1,0:T(8,128)} %bitcast.8, s32[16,192]{1,0:T(8,128)} %bitcast.9, s32[192]{0:T(256)} %target.1, bf16[128,128,128]{2,1,0:T(8,128)(2,1)} %bitcast.6, bf16[128,128,128]{2,1,0:T(8,128)(2,1)} %bitcast.7), custom_call_target="tpu_custom_call" | custom-call | flops 12884901888 | bytes 25165824 | tf_op jit(solution)/shard_map/pallas_call | solution.py:59
  44.2 234.8 %shard_map.65 = f32[4,32,32,128]{3,2,1,0:T(8,128)} custom-call(f32[4,4]{1,0:T(4,128)} %weights.1, f32[4,2,16,4,2,32,128]{6,5,4,3,2,1,0:T(8,128)} %bitcast.5), custom_call_target="tpu_custom_call" | custom-call | tf_op jit(solution)/shard_map/pallas_call | solution.py:307
  279.1 3.1 %copy.8 = f32[4,32,32,128]{3,2,1,0:T(8,128)} copy(f32[4,32,32,128]{3,2,1,0:T(8,128)} %shard_map.65) | data formatting | bytes 4194304
